TPU v7x, 32 devices: a whole 2x2x4 slice. The times are simulated.
32 devices in a mesh: dp: 4 (over x, core), ep: 8 (over z, y).
Axes of the slice: x: 2, y: 2, z: 4, core: 2. Of those that a mesh axis runs over, the one named last changes fastest.
Arguments:
- tokens: bfloat16 [4096, 7168], P(('dp', 'ep')), may hold values from -6 to 6
- out_grad: bfloat16 [4096, 7168], P(('dp', 'ep')), may hold values from -3 to 3
- expert_ids: int32 [4096, 8], P(('dp', 'ep')), may hold values from 0 to 255, as said below
- route_weights: bfloat16 [4096, 8], P(('dp', 'ep')), may hold values from 0.099609375 to 1
- gate_matrix: bfloat16 [7168, 2048], P('dp', 'ep'), may hold values from -0.0625 to 0.0625
- up_matrix: bfloat16 [7168, 2048], P('dp', 'ep'), may hold values from -0.0625 to 0.0625
- down_matrix: bfloat16 [7168, 2048], P('dp', 'ep'), may hold values from -0.125 to 0.125
Outputs:
- input_gradient: bfloat16 [4096, 7168], P(('dp', 'ep'))
- route_gradient: float32 [4096, 8], P(('dp', 'ep'))
- gate_gradient: bfloat16 [7168, 2048], P('dp', 'ep')
- up_gradient: bfloat16 [7168, 2048], P('dp', 'ep')
- down_gradient: bfloat16 [7168, 2048], P('dp', 'ep')
Inputs may be any that keep to these rules, and one draw needn't show every extreme that they name: `expert_ids`: each row names 8 different ids, 2 in each of 4 groups of 32 consecutive ids. In each aligned block of 1024 rows, one id that is a multiple of 256 is named by 8 or more rows of every aligned block of 128 rows inside it.
All inputs are finite; a program needn't handle non-finite values.
Results may differ from a plain program's by a relative error of at most 0.014.
Values may be sent and summed in bfloat16 or wider, within the bound.
A program may use at most 128 MiB of HBM per device.

v0:
```python
import jax
import jax.numpy as jnp
from jax import lax
from jax.sharding import PartitionSpec as P

ROUTED = 256
TOPK = 8
SLICES = 8
CAP = 8


def hidden_terms(gate_pre, up_pre, projected, gate_rows):
    sigmoid = jax.nn.sigmoid(gate_pre)
    swished = gate_pre * sigmoid
    hidden = lax.optimization_barrier((swished * up_pre).astype(jnp.bfloat16)).astype(jnp.float32)
    route_part = jnp.sum(hidden * projected, axis=1).astype(jnp.bfloat16)
    scaling = gate_rows.astype(jnp.float32)[:, None]
    grad_hidden = scaling * projected
    gate_delta = grad_hidden * up_pre * sigmoid * (1.0 + gate_pre * (1.0 - sigmoid))
    up_delta = grad_hidden * swished
    deltas = jnp.concatenate([gate_delta, up_delta], axis=1).astype(jnp.bfloat16)
    scaled = (scaling * hidden).astype(jnp.bfloat16)
    return (deltas, scaled, route_part)


def body(tokens, out_grad, expert_ids, route_weights, gate_matrix, up_matrix, down_matrix):
    senders = lax.axis_size("ep")
    experts = senders // SLICES
    stride = ROUTED // experts
    tok_rows = tokens.shape[0]
    width = tokens.shape[1]
    local_width = gate_matrix.shape[0]
    hid_width = gate_matrix.shape[1]
    flat_ids = expert_ids.reshape(tok_rows * TOPK)
    window = flat_ids % stride == 0
    expert = jnp.where(window, flat_ids // stride, experts)
    column = jnp.arange(experts, dtype=jnp.int32)
    onehot = (expert[:, None] == column[None, :]).astype(jnp.int32)
    earlier = jnp.cumsum(onehot, axis=0) - onehot
    slot_index = jnp.sum(earlier * onehot, axis=1)
    kept_entry = window & (slot_index < CAP)
    places = jnp.arange(experts * CAP, dtype=jnp.int32)
    assign = kept_entry[:, None] & ((expert * CAP + slot_index)[:, None] == places[None, :])
    assign = assign.astype(jnp.float32).reshape(tok_rows, TOPK, experts * CAP)
    select = jnp.sum(assign, axis=1).astype(jnp.bfloat16)
    slot_in = jnp.einsum("ts,td->sd", select, tokens, preferred_element_type=jnp.float32).astype(
        jnp.bfloat16
    )
    slot_grad = jnp.einsum(
        "ts,td->sd", select, out_grad, preferred_element_type=jnp.float32
    ).astype(jnp.bfloat16)
    slot_gate = jnp.einsum(
        "tks,tk->s", assign, route_weights.astype(jnp.float32), precision=lax.Precision.HIGHEST
    ).astype(jnp.bfloat16)
    send_in = jnp.repeat(slot_in.reshape(experts, CAP, width), SLICES, axis=0)
    send_grad = jnp.repeat(slot_grad.reshape(experts, CAP, width), SLICES, axis=0)
    send_gate = jnp.repeat(slot_gate.reshape(experts, CAP), SLICES, axis=0)
    rows_in, rows_grad, rows_gate = (
        lax.all_to_all(send_in, "ep", split_axis=0, concat_axis=0, tiled=True),
        lax.all_to_all(send_grad, "ep", split_axis=0, concat_axis=0, tiled=True),
        lax.all_to_all(send_gate, "ep", split_axis=0, concat_axis=0, tiled=True),
    )
    total_rows = senders * CAP
    rows_in = rows_in.reshape(total_rows, width)
    rows_grad = rows_grad.reshape(total_rows, width)
    rows_gate = rows_gate.reshape(total_rows)
    stacked = jnp.concatenate([gate_matrix, up_matrix], axis=1)
    groups = lax.axis_size("dp")
    all_in, all_grad = (
        lax.all_to_all(rows_in, "dp", split_axis=1, concat_axis=0, tiled=True),
        lax.all_to_all(rows_grad, "dp", split_axis=1, concat_axis=0, tiled=True),
    )
    part_in = all_in
    part_grad = all_grad
    first = jnp.dot(part_in, stacked, preferred_element_type=jnp.float32)
    second = jnp.dot(part_grad, down_matrix, preferred_element_type=jnp.float32)
    own_sums = lax.psum_scatter(
        jnp.concatenate([first, second], axis=1), "dp", scatter_dimension=0, tiled=True
    )
    deltas, scaled, route_part = hidden_terms(
        own_sums[:, :hid_width],
        own_sums[:, hid_width : 2 * hid_width],
        own_sums[:, 2 * hid_width :],
        rows_gate,
    )
    group_in = all_in.reshape(groups, total_rows, local_width)
    group_grad = all_grad.reshape(groups, total_rows, local_width)
    piece_deltas = lax.all_gather(
        deltas.reshape(1, total_rows, 2 * hid_width), "dp", axis=0, tiled=True
    )
    piece_scaled = lax.all_gather(
        scaled.reshape(1, total_rows, hid_width), "dp", axis=0, tiled=True
    )
    part_in = group_in
    part_grad = group_grad
    left = jnp.einsum("grd,grh->gdh", part_in, piece_deltas, preferred_element_type=jnp.float32)
    right = jnp.einsum("grd,grh->gdh", part_grad, piece_scaled, preferred_element_type=jnp.float32)
    pair_total = jnp.sum(
        lax.optimization_barrier(left.astype(jnp.bfloat16)).astype(jnp.float32), axis=0
    )
    down_total = jnp.sum(
        lax.optimization_barrier(right.astype(jnp.bfloat16)).astype(jnp.float32), axis=0
    )
    rows_part = jnp.einsum(
        "grh,dh->grd", piece_deltas, stacked, preferred_element_type=jnp.float32
    ).astype(jnp.bfloat16)
    input_all = rows_part
    pair_total, down_total, input_all = (pair_total, down_total, input_all)
    partial_value = lax.all_to_all(
        input_all.reshape(groups * total_rows, local_width),
        "dp",
        split_axis=0,
        concat_axis=1,
        tiled=True,
    )
    summed = jnp.concatenate([pair_total, down_total], axis=1)
    back_in, back_route = (
        lax.all_to_all(
            partial_value.reshape(senders, CAP, width),
            "ep",
            split_axis=0,
            concat_axis=0,
            tiled=True,
        ),
        lax.all_to_all(
            route_part.reshape(senders, CAP), "ep", split_axis=0, concat_axis=0, tiled=True
        ),
    )
    slot_sums = jnp.sum(
        back_in.reshape(experts, SLICES, CAP, width).astype(jnp.float32), axis=1
    ).reshape(experts * CAP, width)
    route_sums = jnp.sum(
        back_route.reshape(experts, SLICES, CAP).astype(jnp.float32), axis=1
    ).reshape(experts * CAP)
    input_gradient = jnp.dot(
        select.astype(jnp.float32), slot_sums, precision=lax.Precision.HIGHEST
    ).astype(jnp.bfloat16)
    route_gradient = jnp.einsum("tks,s->tk", assign, route_sums, precision=lax.Precision.HIGHEST)
    gate_gradient = summed[:, :hid_width].astype(jnp.bfloat16)
    up_gradient = summed[:, hid_width : 2 * hid_width].astype(jnp.bfloat16)
    down_gradient = summed[:, 2 * hid_width :].astype(jnp.bfloat16)
    return (input_gradient, route_gradient, gate_gradient, up_gradient, down_gradient)


def solution(mesh):
    return jax.shard_map(
        body,
        mesh=mesh,
        in_specs=(
            P(("dp", "ep"), None),
            P(("dp", "ep"), None),
            P(("dp", "ep"), None),
            P(("dp", "ep"), None),
            P("dp", "ep"),
            P("dp", "ep"),
            P("dp", "ep"),
        ),
        out_specs=(
            P(("dp", "ep"), None),
            P(("dp", "ep"), None),
            P("dp", "ep"),
            P("dp", "ep"),
            P("dp", "ep"),
        ),
        check_vma=False,
    )
```

profile of v0, /device:TPU:0, one launch (start us, length us, event | category | flops | bytes accessed | tf_op | source)
XLA Modules:
  0.0 214.9 jit_solution(8811505149957647940)
XLA Ops:
  7.2 0.0 copy-start
  7.2 0.9 copy.47
  8.1 0.1 reshape.441
  8.2 0.3 reduce-window.6
  8.5 0.2 slice_reduce_fusion
  8.7 0.1 reshape.442
  8.8 0.2 reduce-window.9
  9.0 0.1 broadcast.333
  9.0 0.1 reshape.445
  9.2 0.1 copy.48
  9.2 0.7 compare_and_fusion
  10.0 0.7 multiply_add_fusion
  10.7 0.3 convolution_convert_fusion.1
  11.0 1.0 reshape.448
  12.0 7.3 %all-to-all-start.3 = ((bf16[8,8,7168]{2,1,0:T(8,128)(2,1)}), bf16[8,8,7168]{2,1,0:T(8,128)(2,1)S(1)}, u32[]{:S(2)}, u32[]{:S(2)}) async-start(bf16[8,8,7168]{2,1,0:T(8,128)(2,1)} %reshape.448), calls=%async_computation.3 | async-start | bytes 1835008 | tf_op jit(solution)/shard_map/all_to_all | solution.py:60
  19.4 1.8 convolution_convert_fusion.2
  21.2 21.2 %all-to-all-done.3 = bf16[8,8,7168]{2,1,0:T(8,128)(2,1)S(1)} async-done(((bf16[8,8,7168]{2,1,0:T(8,128)(2,1)}), bf16[8,8,7168]{2,1,0:T(8,128)(2,1)S(1)}, u32[]{:S(2)}, u32[]{:S(2)}) %all-to-all-start.3) | async-done | bytes 917536 | tf_op jit(solution)/shard_map/all_to_all | solution.py:60
  42.4 1.0 reshape.447
  43.4 0.2 copy-done.4
  43.6 3.6 %all-to-all-start.1 = ((bf16[8,8,7168]{2,1,0:T(8,128)(2,1)}), bf16[8,8,7168]{2,1,0:T(8,128)(2,1)S(1)}, u32[]{:S(2)}, u32[]{:S(2)}) async-start(bf16[8,8,7168]{2,1,0:T(8,128)(2,1)} %reshape.447), calls=%async_computation.1 | async-start | bytes 1835008 | tf_op jit(solution)/shard_map/all_to_all | solution.py:59
  47.2 2.9 %all_to_all.62 = bf16[64,4,1792]{2,1,0:T(4,128)(2,1)} reshape(bf16[8,8,7168]{2,1,0:T(8,128)(2,1)} %copy-done.4) | data formatting | bytes 1835008 | tf_op jit(solution)/shard_map/all_to_all | solution.py:71
  50.0 2.2 %copy.51 = bf16[64,4,1792]{2,0,1:T(8,128)(2,1)} copy(bf16[64,4,1792]{2,1,0:T(4,128)(2,1)} %all_to_all.62) | data formatting | bytes 1835008 | tf_op jit(solution)/shard_map/all_to_all | solution.py:71
  52.2 18.0 %all-to-all-done.1 = bf16[8,8,7168]{2,1,0:T(8,128)(2,1)S(1)} async-done(((bf16[8,8,7168]{2,1,0:T(8,128)(2,1)}), bf16[8,8,7168]{2,1,0:T(8,128)(2,1)S(1)}, u32[]{:S(2)}, u32[]{:S(2)}) %all-to-all-start.1) | async-done | bytes 917536 | tf_op jit(solution)/shard_map/all_to_all | solution.py:59
  70.3 0.9 copy-done.3
  71.2 3.5 %all-to-all-start.4 = ((bf16[64,4,1792]{2,0,1:T(8,128)(2,1)}), bf16[64,4,1792]{2,0,1:T(8,128)(2,1)S(1)}, u32[]{:S(2)}, u32[]{:S(2)}) async-start(bf16[64,4,1792]{2,0,1:T(8,128)(2,1)} %copy.51), calls=%async_computation.4 | async-start | bytes 1835008 | tf_op jit(solution)/shard_map/all_to_all | solution.py:71
  74.7 2.9 %all_to_all.57 = bf16[64,4,1792]{2,1,0:T(4,128)(2,1)} reshape(bf16[8,8,7168]{2,1,0:T(8,128)(2,1)} %copy-done.3) | data formatting | bytes 1835008 | tf_op jit(solution)/shard_map/all_to_all | solution.py:70
  77.6 2.2 %copy.50 = bf16[64,4,1792]{2,0,1:T(8,128)(2,1)} copy(bf16[64,4,1792]{2,1,0:T(4,128)(2,1)} %all_to_all.57) | data formatting | bytes 1835008 | tf_op jit(solution)/shard_map/all_to_all | solution.py:70
  79.8 7.9 %all-to-all-done.4 = bf16[64,4,1792]{2,0,1:T(8,128)(2,1)S(1)} async-done(((bf16[64,4,1792]{2,0,1:T(8,128)(2,1)}), bf16[64,4,1792]{2,0,1:T(8,128)(2,1)S(1)}, u32[]{:S(2)}, u32[]{:S(2)}) %all-to-all-start.4) | async-done | bytes 917536 | tf_op jit(solution)/shard_map/all_to_all | solution.py:71
  87.7 0.9 copy-done.1
  88.6 3.5 %all-to-all-start.2 = ((bf16[64,4,1792]{2,0,1:T(8,128)(2,1)}), bf16[64,4,1792]{2,0,1:T(8,128)(2,1)S(1)}, u32[]{:S(2)}, u32[]{:S(2)}) async-start(bf16[64,4,1792]{2,0,1:T(8,128)(2,1)} %copy.50), calls=%async_computation.2 | async-start | bytes 1835008 | tf_op jit(solution)/shard_map/all_to_all | solution.py:70
  92.1 0.0 reduce-scatter.2.cloned.1.call-start
  92.2 0.0 copy-start.5
  92.2 2.3 %constant_dynamic-update-slice_fusion.1 = bf16[1792,512]{1,0:T(8,128)(2,1)} fusion(bf16[1792,256]{1,0:T(8,128)(2,1)} %param.11), kind=kLoop, calls=%fused_computation.35 | loop fusion | bytes 1835008
  94.5 1.0 constant_dynamic-update-slice_fusion
  95.5 0.4 fusion.34
  95.9 9.2 %all-to-all-done.2 = bf16[64,4,1792]{2,0,1:T(8,128)(2,1)S(1)} async-done(((bf16[64,4,1792]{2,0,1:T(8,128)(2,1)}), bf16[64,4,1792]{2,0,1:T(8,128)(2,1)S(1)}, u32[]{:S(2)}, u32[]{:S(2)}) %all-to-all-start.2) | async-done | bytes 917536 | tf_op jit(solution)/shard_map/all_to_all | solution.py:70
  105.1 2.1 fusion.33
  107.3 0.9 pad_maximum_fusion
  108.2 0.0 reduce-scatter.2.cloned.1.call-update
  108.2 0.1 fusion.1
  108.4 9.9 %all_to_all.78 = bf16[8,1,8]{2,1,0:T(2,128)(2,1)S(1)} all-to-all(bf16[8,1,8]{2,1,0:T(2,128)(2,1)S(1)} %reshape.446), channel_id=1, replica_groups=mesh['dp'=4,'ep'=8] {'ep'}, dimensions={0} | all-to-all | bytes 256 | tf_op jit(solution)/shard_map/all_to_all | solution.py:61
  118.3 0.1 reshape.451
  118.4 11.3 %reduce-scatter.2.cloned.1.call-done = f32[64,768]{1,0:T(8,128)} async-done(((f32[256,768]{1,0:T(8,128)}), f32[64,768]{1,0:T(8,128)}) %reduce-scatter.2.cloned.1.call-update) | async-done | bytes 196624 | tf_op jit(solution)/shard_map/reduce_scatter | solution.py:77
  129.7 0.9 multiply_convert_fusion
  130.6 1.1 fusion.11
  131.7 5.8 %all_gather.6 = bf16[4,64,512]{2,1,0:T(8,128)(2,1)S(1)} all-gather(bf16[1,64,512]{2,1,0:T(8,128)(2,1)S(1)} %pad_maximum_fusion.1), channel_id=1, replica_groups=mesh['dp'=4,'ep'=8] {'dp'}, dimensions={0}, use_global_device_ids=true | all-gather | bytes 327680 | tf_op jit(solution)/shard_map/all_gather | solution.py:88
  137.5 3.1 %convolution_convert_fusion.5 = bf16[4,64,1792]{2,1,0:T(8,128)(2,1)} fusion(bf16[4,64,512]{2,1,0:T(8,128)(2,1)S(1)} %all_gather.6, bf16[1792,512]{1,0:T(8,128)(2,1)} %constant_dynamic-update-slice_fusion), kind=kOutput, calls=%fused_computation.5 | convolution fusion | flops 470220800 | bytes 3014656 | tf_op jit(solution)/shard_map/grh,dh->grd/dot_general | solution.py:104
  140.6 4.2 %all-to-all-start.5 = ((bf16[4,64,1792]{2,1,0:T(8,128)(2,1)}), bf16[4,64,1792]{2,1,0:T(8,128)(2,1)}, u32[]{:S(2)}, u32[]{:S(2)}) async-start(bf16[4,64,1792]{2,1,0:T(8,128)(2,1)} %convolution_convert_fusion.5), calls=%async_computation.6 | async-start | bytes 1835008 | tf_op jit(solution)/shard_map/all_to_all | solution.py:109
  144.8 0.7 convert_element_type.139
  145.5 12.4 %all-to-all-done.5 = bf16[4,64,1792]{2,1,0:T(8,128)(2,1)} async-done(((bf16[4,64,1792]{2,1,0:T(8,128)(2,1)}), bf16[4,64,1792]{2,1,0:T(8,128)(2,1)}, u32[]{:S(2)}, u32[]{:S(2)}) %all-to-all-start.5) | async-done | bytes 917536 | tf_op jit(solution)/shard_map/all_to_all | solution.py:109
  157.9 5.5 %all-to-all-start.7 = ((bf16[8,1,8]{2,1,0:T(2,128)(2,1)}), bf16[8,1,8]{2,1,0:T(2,128)(2,1)S(1)}, u32[]{:S(2)}, u32[]{:S(2)}) async-start(bf16[8,1,8]{2,1,0:T(2,128)(2,1)} %convert_element_type.139), calls=%async_computation.8 | async-start | bytes 8192 | tf_op jit(solution)/shard_map/all_to_all | solution.py:125
  163.4 5.4 %all-gather = bf16[256,256]{1,0:T(8,128)(2,1)S(1)} all-gather(bf16[64,256]{1,0:T(8,128)(2,1)S(1)} %get-tuple-element.10), channel_id=2, replica_groups=mesh['dp'=4,'ep'=8] {'dp'}, dimensions={0}, use_global_device_ids=true | all-gather | bytes 163840 | tf_op jit(solution)/shard_map/all_gather | solution.py:91
  168.8 2.8 %copy.53 = bf16[64,4,1792]{2,1,0:T(4,128)(2,1)} copy(bf16[64,4,1792]{2,0,1:T(8,128)(2,1)} %bitcast.10) | data formatting | bytes 1835008 | tf_op jit(solution)/shard_map/all_to_all | solution.py:109
  171.6 2.7 %reshape.449 = bf16[8,8,7168]{2,1,0:T(8,128)(2,1)} reshape(bf16[64,4,1792]{2,1,0:T(4,128)(2,1)} %copy.53) | data formatting | bytes 1835008 | tf_op jit(solution)/shard_map/reshape | solution.py:119
  174.3 6.0 %all-to-all-start.6 = ((bf16[8,8,7168]{2,1,0:T(8,128)(2,1)}), bf16[8,8,7168]{2,1,0:T(8,128)(2,1)}, u32[]{:S(2)}, u32[]{:S(2)}) async-start(bf16[8,8,7168]{2,1,0:T(8,128)(2,1)} %reshape.449), calls=%async_computation.7 | async-start | bytes 1835008 | tf_op jit(solution)/shard_map/all_to_all | solution.py:118
  180.3 4.2 %convolution_convert_fusion.4 = bf16[4,1792,256]{2,1,0:T(8,128)(2,1)} fusion(bf16[4,64,256]{2,1,0:T(8,128)(2,1)S(1)} %bitcast.50, bf16[64,4,1792]{2,0,1:T(8,128)(2,1)} %copy-done.1), kind=kOutput, calls=%fused_computation.4 | convolution fusion | flops 236716032 | bytes 4718592 | tf_op jit(solution)/shard_map/grd,grh->gdh/dot_general | solution.py:97
  184.6 5.1 %convolution_convert_fusion.3 = bf16[4,1792,512]{2,1,0:T(8,128)(2,1)} fusion(bf16[4,64,512]{2,1,0:T(8,128)(2,1)S(1)} %all_gather.6, bf16[64,4,1792]{2,0,1:T(8,128)(2,1)S(1)} %all-to-all-done.2), kind=kOutput, calls=%fused_computation.3 | convolution fusion | flops 473432064 | bytes 8519680 | tf_op jit(solution)/shard_map/grd,grh->gdh/dot_general | solution.py:96
  189.7 3.8 %reduce_sum.66 = bf16[1792,256]{1,0:T(8,128)(2,1)} reduce(bf16[4,1792,256]{2,1,0:T(8,128)(2,1)} %convolution_convert_fusion.4, bf16[]{:T(256)} %constant.44.clone.1), dimensions={0}, to_apply=%region_8.9 | reduce | flops 1376256 | bytes 4587522 | tf_op jit(solution)/shard_map/reduce_sum | solution.py:101
  193.4 6.0 %reduce.5 = bf16[1792,512]{1,0:T(8,128)(2,1)} reduce(bf16[4,1792,512]{2,1,0:T(8,128)(2,1)} %convolution_convert_fusion.3, bf16[]{:T(256)} %constant.44.clone.1), dimensions={0}, to_apply=%region_7.8.clone | reduce | flops 2752512 | bytes 9175042 | tf_op jit(solution)/shard_map/reduce_sum | solution.py:98
  199.4 2.8 %fusion.32 = (bf16[1792,256]{1,0:T(8,128)(2,1)}, bf16[1792,256]{1,0:T(8,128)(2,1)}) fusion(bf16[1792,512]{1,0:T(8,128)(2,1)} %reduce.5), kind=kLoop, calls=%fused_computation.70 | loop fusion | bytes 3670016 | tf_op jit(solution)/shard_map/slice | solution.py:140
  202.2 0.7 fusion.13
  203.0 0.9 all-to-all-done.6
  203.9 1.3 convert_reduce_fusion
  205.2 2.9 %convolution_convert_fusion = bf16[128,7168]{1,0:T(8,128)(2,1)} fusion(f32[8,7168]{1,0:T(8,128)S(1)} %convert_reduce_fusion, bf16[128,8]{0,1:T(8,128)(2,1)S(1)} %convert_reduce_fusion.1), kind=kOutput, calls=%fused_computation | convolution fusion | flops 88997888 | bytes 2066432 | tf_op jit(solution)/shard_map/dot_general | solution.py:135
  (20 shorter events, 0.2 us)
Async XLA Ops:
  7.2 3.5 %copy-start = (bf16[128,7168]{1,0:T(8,128)(2,1)S(1)}, bf16[128,7168]{1,0:T(8,128)(2,1)}, u32[]{:S(2)}) copy-start(bf16[128,7168]{1,0:T(8,128)(2,1)} %param.8) | copy-start | bytes 5505028
  12.0 30.3 %all-to-all-start.3 = ((bf16[8,8,7168]{2,1,0:T(8,128)(2,1)}), bf16[8,8,7168]{2,1,0:T(8,128)(2,1)S(1)}, u32[]{:S(2)}, u32[]{:S(2)}) async-start(bf16[8,8,7168]{2,1,0:T(8,128)(2,1)} %reshape.448), calls=%async_computation.3 | async-start | bytes 1835008 | tf_op jit(solution)/shard_map/all_to_all | solution.py:60
  42.4 1.2 copy-start.4
  43.6 26.7 %all-to-all-start.1 = ((bf16[8,8,7168]{2,1,0:T(8,128)(2,1)}), bf16[8,8,7168]{2,1,0:T(8,128)(2,1)S(1)}, u32[]{:S(2)}, u32[]{:S(2)}) async-start(bf16[8,8,7168]{2,1,0:T(8,128)(2,1)} %reshape.447), calls=%async_computation.1 | async-start | bytes 1835008 | tf_op jit(solution)/shard_map/all_to_all | solution.py:59
  70.3 0.9 copy-start.3
  71.2 16.5 %all-to-all-start.4 = ((bf16[64,4,1792]{2,0,1:T(8,128)(2,1)}), bf16[64,4,1792]{2,0,1:T(8,128)(2,1)S(1)}, u32[]{:S(2)}, u32[]{:S(2)}) async-start(bf16[64,4,1792]{2,0,1:T(8,128)(2,1)} %copy.51), calls=%async_computation.4 | async-start | bytes 1835008 | tf_op jit(solution)/shard_map/all_to_all | solution.py:71
  87.7 0.9 copy-start.1
  88.6 16.5 %all-to-all-start.2 = ((bf16[64,4,1792]{2,0,1:T(8,128)(2,1)}), bf16[64,4,1792]{2,0,1:T(8,128)(2,1)S(1)}, u32[]{:S(2)}, u32[]{:S(2)}) async-start(bf16[64,4,1792]{2,0,1:T(8,128)(2,1)} %copy.50), calls=%async_computation.2 | async-start | bytes 1835008 | tf_op jit(solution)/shard_map/all_to_all | solution.py:70
  92.1 37.6 %reduce-scatter.2.cloned.1.call-start = ((), (), s32[]{:S(2)}) async-start(), calls=%async_computation.9 | async-start | bytes 983040 | tf_op jit(solution)/shard_map/reduce_scatter | solution.py:77
  92.2 2.4 %copy-start.5 = (bf16[1792,256]{1,0:T(8,128)(2,1)S(1)}, bf16[1792,256]{1,0:T(8,128)(2,1)}, u32[]{:S(2)}) copy-start(bf16[1792,256]{1,0:T(8,128)(2,1)} %param.12) | copy-start | bytes 2752516
  92.2 3.3 %copy-start.2 = (bf16[64,4,1792]{2,0,1:T(8,128)(2,1)S(1)}, bf16[64,4,1792]{2,0,1:T(8,128)(2,1)}, u32[]{:S(2)}) copy-start(bf16[64,4,1792]{2,0,1:T(8,128)(2,1)} %copy-done.1) | copy-start | bytes 2752516
  92.2 3.3 %copy-start.6 = (bf16[1792,256]{1,0:T(8,128)(2,1)S(1)}, bf16[1792,256]{1,0:T(8,128)(2,1)}, u32[]{:S(2)}) copy-start(bf16[1792,256]{1,0:T(8,128)(2,1)} %param.13) | copy-start | bytes 2752516
  107.3 1.0 copy-start.7
  140.6 17.3 %all-to-all-start.5 = ((bf16[4,64,1792]{2,1,0:T(8,128)(2,1)}), bf16[4,64,1792]{2,1,0:T(8,128)(2,1)}, u32[]{:S(2)}, u32[]{:S(2)}) async-start(bf16[4,64,1792]{2,1,0:T(8,128)(2,1)} %convolution_convert_fusion.5), calls=%async_computation.6 | async-start | bytes 1835008 | tf_op jit(solution)/shard_map/all_to_all | solution.py:109
  157.9 16.4 %all-to-all-start.7 = ((bf16[8,1,8]{2,1,0:T(2,128)(2,1)}), bf16[8,1,8]{2,1,0:T(2,128)(2,1)S(1)}, u32[]{:S(2)}, u32[]{:S(2)}) async-start(bf16[8,1,8]{2,1,0:T(2,128)(2,1)} %convert_element_type.139), calls=%async_computation.8 | async-start | bytes 8192 | tf_op jit(solution)/shard_map/all_to_all | solution.py:125
  174.3 29.6 %all-to-all-start.6 = ((bf16[8,8,7168]{2,1,0:T(8,128)(2,1)}), bf16[8,8,7168]{2,1,0:T(8,128)(2,1)}, u32[]{:S(2)}, u32[]{:S(2)}) async-start(bf16[8,8,7168]{2,1,0:T(8,128)(2,1)} %reshape.449), calls=%async_computation.7 | async-start | bytes 1835008 | tf_op jit(solution)/shard_map/all_to_all | solution.py:118
Sparse Core Ops, SparseCore 0:
  108.4 21.3 reduce-scatter.1
where the time goes:
time: 216 us; the launch traced here: 215 us
  waiting for transfers between devices  81 us (38%)
  starting transfers between devices  33.6 us (16%)
  local copies, waits for them, and re-layouts  28.2 us (13%)
  blocking collectives  21.1 us (10%)
  matrix products  20.9 us (10%)
  other arithmetic  16 us (7%)
  between operations  14.2 us (7%)
    all_to_all x1, waiting for transfers between devices, body(): lax.all_to_all(send_grad, 'ep', split_axis=0, concat_axis=0, tiled=True)  21.2 us
    all_to_all x1, waiting for transfers between devices, body(): lax.all_to_all(send_in, 'ep', split_axis=0, concat_axis=0, tiled=True)  18 us
    all_to_all x1, waiting for transfers between devices, body(): lax.all_to_all(input_all.reshape(groups * total_rows, local_width), 'dp',...  12.4 us
    reduce_scatter x1, waiting for transfers between devices, body(): lax.psum_scatter(jnp.concatenate([first, second], axis=1), 'dp', scatter_...  11.3 us
    all_to_all x1, blocking collectives, body(): lax.all_to_all(send_gate, 'ep', split_axis=0, concat_axis=0, tiled=True)  9.92 us
    all_to_all x1, waiting for transfers between devices, body(): lax.all_to_all(rows_in, 'dp', split_axis=1, concat_axis=0, tiled=True)  9.19 us
    all_to_all x1, waiting for transfers between devices, body(): lax.all_to_all(rows_grad, 'dp', split_axis=1, concat_axis=0, tiled=True)  7.92 us
    all_to_all x1, starting transfers between devices, body(): lax.all_to_all(send_grad, 'ep', split_axis=0, concat_axis=0, tiled=True)  7.31 us
  transfers between devices with their start and end apart: 8, of which 7 were waited for; matrix products, arithmetic and copies ran while one was open for 18% of the time, Pallas kernels for 0%

commit v1 on v0

v1 whole, which is shorter than its diff:
```python
import functools
import jax
import jax.numpy as jnp
from jax import lax
from jax.experimental import pallas as pl
from jax.experimental.pallas import tpu as pltpu
from jax.sharding import PartitionSpec as P

ROUTED = 256
TOPK = 8
SLICES = 8
CAP = 8
LANES = 128
BF = jnp.bfloat16
F32 = jnp.float32
MESH = pl.DeviceIdType.MESH


def kernel(
    n_dp, n_ep,
    tok_hbm, grad_hbm, ids_ref, rw_ref, a_hbm, b_hbm, c_hbm,
    ig_hbm, rg_ref, ga_hbm, gb_hbm, gc_hbm,
    tokbuf, gradbuf, wab, wc, send1, shard, ag, xs, ys, gates, psum, arsend, arrecv,
    deltas, scaleds, rp, r1recv, r2send, r2recv, retbuf, fin, ga, gb, gc,
    in_sem, w_sem, out_sem, s1s, s1r, s2s, s2r, s3s, s3r, ars, arr, r1s, r1r, r2s, r2r, fs, fr,
):
    experts = n_ep // SLICES
    stride = ROUTED // experts
    places = experts * CAP
    n_hi = n_ep // 2
    rows, width = tok_hbm.shape
    lw, hid = a_hbm.shape
    nb = n_dp.bit_length() - 1
    chunk = 2 * n_dp * CAP
    half = n_dp * CAP
    g = lax.axis_index("dp")
    e = lax.axis_index("ep")
    hi, lo = e // 2, e % 2
    other = hi * 2 + (1 - lo)
    mine_w = e // SLICES

    def rc(src, dst, ss, rs, **where):
        return pltpu.make_async_remote_copy(
            src_ref=src, dst_ref=dst, send_sem=ss, recv_sem=rs,
            device_id=where, device_id_type=MESH)

    def cols(j):
        gp = lax.rem(g + j, n_dp)
        return gp, pl.ds(pl.multiple_of(gp * lw, LANES), lw)

    loads = []
    order = list(range(1, n_dp)) + [0]
    for j in order:
        gp, ds = cols(j)
        c1 = pltpu.make_async_copy(tok_hbm.at[:, ds], tokbuf.at[j], in_sem.at[0, j])
        c2 = pltpu.make_async_copy(grad_hbm.at[:, ds], gradbuf.at[j], in_sem.at[1, j])
        c1.start()
        c2.start()
        loads.append((j, gp, c1, c2))
    wloads = [
        pltpu.make_async_copy(a_hbm, wab.at[:, pl.ds(0, hid)], w_sem.at[0]),
        pltpu.make_async_copy(b_hbm, wab.at[:, pl.ds(hid, hid)], w_sem.at[1]),
        pltpu.make_async_copy(c_hbm, wc, w_sem.at[2]),
    ]
    for c in wloads:
        c.start()

    barrier = pltpu.get_barrier_semaphore()
    for j in range(1, n_dp):
        pl.semaphore_signal(barrier, inc=1, device_id={"dp": lax.rem(g + j, n_dp)}, device_id_type=MESH)
    for j in range(1, n_hi):
        pl.semaphore_signal(
            barrier, inc=1, device_id={"ep": lax.rem(hi + j, n_hi) * 2 + lo}, device_id_type=MESH)
    pl.semaphore_signal(barrier, inc=1, device_id={"ep": other}, device_id_type=MESH)

    ids = ids_ref[...]
    rw = rw_ref[...].astype(F32)
    lane = lax.broadcasted_iota(jnp.int32, (rows, LANES), 1)
    wanted = jnp.where(lane < places, (lane // CAP) * stride, -1)
    hits = jnp.zeros((rows, LANES), F32)
    wts = jnp.zeros((rows, LANES), F32)
    for k in range(TOPK):
        m = ids[:, k:k + 1] == wanted
        hits = hits + jnp.where(m, 1.0, 0.0)
        wts = wts + jnp.where(m, rw[:, k:k + 1], 0.0)
    tr = lax.broadcasted_iota(jnp.int32, (rows, rows), 0)
    tc = lax.broadcasted_iota(jnp.int32, (rows, rows), 1)
    lower = jnp.where(tc < tr, 1.0, 0.0).astype(BF)
    slot = jnp.dot(lower, hits.astype(BF), preferred_element_type=F32)
    sel = jnp.where(slot == (lane % CAP).astype(F32), hits, 0.0)
    selT = sel.T[:places].astype(BF)
    gwT = (sel * wts).T[:places].astype(BF)
    gate = jnp.dot(gwT, jnp.ones((rows, LANES), BF), preferred_element_type=F32)
    gate = gate.reshape(experts, CAP, LANES).astype(BF)

    pl.semaphore_wait(barrier, n_dp - 1 + n_hi)

    for j, gp, c1, c2 in loads:
        c1.wait()
        c2.wait()
        xr = jnp.dot(selT, tokbuf[j], preferred_element_type=F32).reshape(experts, CAP, lw).astype(BF)
        yr = jnp.dot(selT, gradbuf[j], preferred_element_type=F32).reshape(experts, CAP, lw).astype(BF)
        if j:
            send1[j, :, :, 0:lw] = xr
            send1[j, :, :, lw:2 * lw] = yr
            send1[j, :, :, 2 * lw:] = gate
            rc(send1.at[j], shard.at[:, g], s1s.at[j], s1r.at[g], dp=gp).start()
        else:
            shard[:, g, :, 0:lw] = xr
            shard[:, g, :, lw:2 * lw] = yr
            shard[:, g, :, 2 * lw:] = gate
    for j in range(1, n_dp):
        src = lax.rem(g + j, n_dp)
        rc(send1.at[j], shard.at[:, src], s1s.at[j], s1r.at[src], dp=src).wait_recv()

    def hop(i):
        h = lax.rem(hi + i, n_hi)
        return rc(shard.at[(h * 2) // SLICES], ag.at[e], s2s.at[h], s2r.at[hi], ep=h * 2 + lo)

    def hop_in(h):
        return rc(shard.at[0], ag.at[h * 2 + lo], s2s.at[h], s2r.at[h], ep=other)

    def fwd(h):
        return rc(ag.at[h * 2 + lo], ag.at[h * 2 + lo], s3s.at[h], s3r.at[h], ep=other)

    def fwd_in(h):
        return rc(ag.at[h * 2 + 1 - lo], ag.at[h * 2 + 1 - lo], s3s.at[h], s3r.at[h], ep=other)

    rc(shard.at[mine_w], ag.at[e], s3s.at[hi], s3r.at[hi], ep=other).start()
    for i in range(1, n_hi):
        hop(i).start()
    ag[e] = shard[mine_w]
    for c in wloads:
        c.wait()

    def ar(b, h):
        bit = 1 << b
        peer = g + (1 - 2 * ((g // bit) % 2)) * bit
        return rc(arsend.at[b, h], arrecv.at[b, h], ars.at[b, h], arr.at[b, h], dp=peer)

    def at_chunk(h):
        return pl.ds(pl.multiple_of(h * chunk, 16), chunk)

    def flow(i, carry):
        @pl.when((i >= 1) & (i < n_hi))
        def _():
            h = lax.rem(hi + i, n_hi)
            hop_in(h).wait_recv()
            fwd(h).start()

        @pl.when((i >= 1) & (i <= n_hi))
        def _():
            h = lax.rem(hi + i - 1, n_hi)
            fwd_in(h).wait_recv()
            got = ag.at[pl.ds(h * 2, 2)]
            x = got[:, :, :, 0:lw].astype(F32).reshape(chunk, lw).astype(BF)
            y = got[:, :, :, lw:2 * lw].astype(F32).reshape(chunk, lw).astype(BF)
            gates[at_chunk(h), :] = got[:, :, :, 2 * lw:].astype(F32).reshape(chunk, LANES)
            xs[at_chunk(h), :] = x
            ys[at_chunk(h), :] = y
            p1 = jnp.dot(x, wab[...], preferred_element_type=F32)
            p2 = jnp.dot(y, wc[...], preferred_element_type=F32)
            psum[h, :, 0:2 * hid] = p1
            psum[h, :, 2 * hid:] = p2
            arsend[0, h, :, 0:2 * hid] = p1.astype(BF)
            arsend[0, h, :, 2 * hid:] = p2.astype(BF)
            ar(0, h).start()

        for b in range(nb - 1):
            @pl.when((i >= 2 + b) & (i < n_hi + 2 + b))
            def _(b=b):
                h = lax.rem(hi + i - 2 - b, n_hi)
                ar(b, h).wait_recv()
                s = psum[h] + arrecv[b, h].astype(F32)
                psum[h] = s
                arsend[b + 1, h] = s.astype(BF)
                ar(b + 1, h).start()
        return carry

    lax.fori_loop(0, n_hi + nb, flow, 0)

    def r1(h):
        return rc(rp.at[h, 1 - lo], r1recv.at[h], r1s.at[h], r1r.at[h], ep=other)

    def finish(i, carry):
        h = lax.rem(hi + i + 1, n_hi)
        ar(nb - 1, h).wait_recv()
        s = psum[h] + arrecv[nb - 1, h].astype(F32)
        gate_pre, up_pre, proj = s[:, :hid], s[:, hid:2 * hid], s[:, 2 * hid:]
        scaling = gates[at_chunk(h), 0:1]
        sig = 1.0 / (1.0 + jnp.exp(-gate_pre))
        sw = gate_pre * sig
        hidden = (sw * up_pre).astype(BF).astype(F32)
        route = jnp.sum(hidden * proj, axis=1, keepdims=True)
        gh = scaling * proj
        d1 = (gh * up_pre * sig * (1.0 + gate_pre * (1.0 - sig))).astype(BF)
        d2 = (gh * sw).astype(BF)
        deltas[at_chunk(h), 0:hid] = d1
        deltas[at_chunk(h), hid:] = d2
        scaleds[at_chunk(h), :] = (scaling * hidden).astype(BF)
        part = lax.dot_general(
            jnp.concatenate([d1, d2], axis=1), wab[...], (((1,), (1,)), ((), ())),
            preferred_element_type=F32)
        rp[h, :, :, 0:lw] = part.reshape(2, half, lw).astype(BF)
        rp[h, :, :, lw:] = jnp.broadcast_to(route, (chunk, LANES)).reshape(2, half, LANES).astype(BF)
        r1(h).start()
        return carry

    lax.fori_loop(0, n_hi, finish, 0)

    def r2(h):
        return rc(r2send.at[h], r2recv.at[hi], r2s.at[h], r2r.at[hi], ep=h * 2 + lo)

    def pair(h):
        r1(h).wait_recv()
        return rp[h, lo].astype(F32) + r1recv[h].astype(F32)

    def combine(i, carry):
        h = lax.rem(hi + i, n_hi)
        r2send[h] = pair(h).astype(BF)
        r2(h).start()
        return carry

    lax.fori_loop(1, n_hi, combine, 0)
    r2recv[hi] = pair(hi).astype(BF)

    tile = 256 if lw % 256 == 0 else 128

    def wgrad(i, carry):
        ds = pl.ds(pl.multiple_of(i * tile, LANES), tile)
        dn = (((0,), (0,)), ((), ()))
        both = lax.dot_general(xs[:, ds], deltas[...], dn, preferred_element_type=F32).astype(BF)
        ga[ds, :] = both[:, :hid]
        gb[ds, :] = both[:, hid:]
        gc[ds, :] = lax.dot_general(ys[:, ds], scaleds[...], dn, preferred_element_type=F32).astype(BF)
        return carry

    lax.fori_loop(0, lw // tile, wgrad, 0)
    outs = [
        pltpu.make_async_copy(ga, ga_hbm, w_sem.at[0]),
        pltpu.make_async_copy(gb, gb_hbm, w_sem.at[1]),
        pltpu.make_async_copy(gc, gc_hbm, w_sem.at[2]),
    ]
    for c in outs:
        c.start()

    for i in range(1, n_hi):
        h = lax.rem(hi + i, n_hi)
        rc(r2send.at[h], r2recv.at[h], r2s.at[h], r2r.at[h], ep=h * 2 + lo).wait_recv()
    per = SLICES // 2
    for w in range(experts):
        acc = r2recv[w * per].astype(F32)
        for j in range(1, per):
            acc = acc + r2recv[w * per + j].astype(F32)
        retbuf[:, w] = acc.reshape(n_dp, CAP, lw + LANES).astype(BF)
    for j in range(1, n_dp):
        gp = lax.rem(g + j, n_dp)
        rc(retbuf.at[gp], fin.at[g], fs.at[j], fr.at[g], dp=gp).start()
    fin[g] = retbuf[g]
    selP = sel[:, :places].astype(BF)
    ocopies = []
    for j in range(n_dp):
        gp, ds = cols(j)
        if j:
            rc(retbuf.at[gp], fin.at[gp], fs.at[j], fr.at[gp], dp=gp).wait_recv()
        vals = fin[gp].astype(F32).reshape(places, lw + LANES)
        if j == 0:
            route = jnp.concatenate(
                [vals[:, lw:], jnp.zeros((LANES - places, LANES), F32)], axis=0).T[0:1]
            lane8 = lax.broadcasted_iota(jnp.int32, (rows, TOPK), 1)
            rg = jnp.zeros((rows, TOPK), F32)
            terms = sel * route
            for k in range(TOPK):
                v = jnp.sum(jnp.where(ids[:, k:k + 1] == wanted, terms, 0.0), axis=1, keepdims=True)
                rg = jnp.where(lane8 == k, v, rg)
            rg_ref[...] = rg
        tokbuf[j] = jnp.dot(selP, vals[:, :lw].astype(BF), preferred_element_type=F32).astype(BF)
        c = pltpu.make_async_copy(tokbuf.at[j], ig_hbm.at[:, ds], out_sem.at[j])
        c.start()
        ocopies.append(c)

    for j in range(1, n_dp):
        gp = lax.rem(g + j, n_dp)
        rc(send1.at[j], shard.at[:, g], s1s.at[j], s1r.at[g], dp=gp).wait_send()
        rc(retbuf.at[gp], fin.at[g], fs.at[j], fr.at[g], dp=gp).wait_send()

    def drain(i, carry):
        h = lax.rem(hi + i, n_hi)
        fwd(h).wait_send()
        for b in range(nb):
            ar(b, h).wait_send()
        r1(h).wait_send()

        @pl.when(i >= 1)
        def _():
            hop(i).wait_send()
            r2(h).wait_send()
        return carry

    lax.fori_loop(0, n_hi, drain, 0)
    for c in outs + ocopies:
        c.wait()


def body(tokens, out_grad, expert_ids, route_weights, gate_matrix, up_matrix, down_matrix):
    n_dp, n_ep = lax.axis_size("dp"), lax.axis_size("ep")
    experts = n_ep // SLICES
    n_hi = n_ep // 2
    rows, width = tokens.shape
    lw, hid = gate_matrix.shape
    nb = n_dp.bit_length() - 1
    chunk = 2 * n_dp * CAP
    half = n_dp * CAP
    total = n_hi * chunk
    C = 2 * lw + LANES
    R = lw + LANES
    V = pltpu.VMEM
    D = lambda *s: pltpu.SemaphoreType.DMA(s)
    anyspec = pl.BlockSpec(memory_space=pl.ANY)
    vspec = pl.BlockSpec(memory_space=pltpu.VMEM)
    return pl.pallas_call(
        functools.partial(kernel, n_dp, n_ep),
        out_shape=(
            jax.ShapeDtypeStruct((rows, width), BF),
            jax.ShapeDtypeStruct((rows, TOPK), F32),
            jax.ShapeDtypeStruct((lw, hid), BF),
            jax.ShapeDtypeStruct((lw, hid), BF),
            jax.ShapeDtypeStruct((lw, hid), BF),
        ),
        in_specs=[anyspec, anyspec, vspec, vspec, anyspec, anyspec, anyspec],
        out_specs=(anyspec, vspec, anyspec, anyspec, anyspec),
        scratch_shapes=[
            V((n_dp, rows, lw), BF), V((n_dp, rows, lw), BF), V((lw, 2 * hid), BF), V((lw, hid), BF),
            V((n_dp, experts, CAP, C), BF), V((experts, n_dp, CAP, C), BF), V((n_ep, n_dp, CAP, C), BF),
            V((total, lw), BF), V((total, lw), BF), V((total, LANES), F32),
            V((n_hi, chunk, 3 * hid), F32), V((nb, n_hi, chunk, 3 * hid), BF), V((nb, n_hi, chunk, 3 * hid), BF),
            V((total, 2 * hid), BF), V((total, hid), BF),
            V((n_hi, 2, half, R), BF), V((n_hi, half, R), BF), V((n_hi, half, R), BF), V((n_hi, half, R), BF),
            V((n_dp, experts, CAP, R), BF), V((n_dp, experts, CAP, R), BF),
            V((lw, hid), BF), V((lw, hid), BF), V((lw, hid), BF),
            D(2, n_dp), D(3), D(n_dp), D(n_dp), D(n_dp), D(n_hi), D(n_hi), D(n_hi), D(n_hi),
            D(nb, n_hi), D(nb, n_hi), D(n_hi), D(n_hi), D(n_hi), D(n_hi), D(n_dp), D(n_dp),
        ],
        compiler_params=pltpu.CompilerParams(
            collective_id=0, has_side_effects=True, vmem_limit_bytes=67043328),
    )(tokens, out_grad, expert_ids, route_weights, gate_matrix, up_matrix, down_matrix)


def solution(mesh):
    return jax.shard_map(
        body,
        mesh=mesh,
        in_specs=(
            P(("dp", "ep"), None),
            P(("dp", "ep"), None),
            P(("dp", "ep"), None),
            P(("dp", "ep"), None),
            P("dp", "ep"),
            P("dp", "ep"),
            P("dp", "ep"),
        ),
        out_specs=(
            P(("dp", "ep"), None),
            P(("dp", "ep"), None),
            P("dp", "ep"),
            P("dp", "ep"),
            P("dp", "ep"),
        ),
        check_vma=False,
    )
```

time: 216 us -> 82.8 us (0.38)
  waiting for transfers between devices: 81 us -> 0 us
  Pallas kernels: 0 us -> 71.3 us
  starting transfers between devices: 33.6 us -> 0 us
  blocking collectives: 21.1 us -> 0 us
  matrix products: 20.9 us -> 0 us
  local copies, waits for them, and re-layouts: 28.2 us -> 10.6 us
  other arithmetic: 16 us -> 0 us
  between operations: 14.2 us -> 0.65 us
    pallas_call x0 -> x1, Pallas kernels: none -> 71.3 us  [body(): pl.pallas_call(functools.partial(kernel, n_dp, n_ep), out_shape=(jax.Shap...]
    all_to_all x7 -> x0, waiting for transfers between devices: 69.7 us -> none  [the longest x1 21.2 us: body(): lax.all_to_all(send_grad, 'ep', split_axis=0, concat_axis=0, tiled=True)]
    all_to_all x7 -> x0, starting transfers between devices: 33.6 us -> none  [the longest x1 7.31 us: body(): lax.all_to_all(send_grad, 'ep', split_axis=0, concat_axis=0, tiled=True)]
    dot_general x10 -> x0, matrix products: 20.9 us -> none  [the longest x1 5.08 us: body(): jnp.einsum('grd,grh->gdh', part_in, piece_deltas, preferred_element_type=...]
    all_to_all x5 -> x0, local copies, waits for them, and re-layouts: 13 us -> none  [the longest x2 5.07 us: body(): lax.all_to_all(rows_in, 'dp', split_axis=1, concat_axis=0, tiled=True)]
    reduce_scatter x1 -> x0, waiting for transfers between devices: 11.3 us -> none  [body(): lax.psum_scatter(jnp.concatenate([first, second], axis=1), 'dp', scatter_...]
    all_gather x2 -> x0, blocking collectives: 11.2 us -> none  [the longest x1 5.78 us: body(): lax.all_gather(deltas.reshape(1, total_rows, 2 * hid_width), 'dp', axis=0...]
    reduce_sum x5 -> x0, other arithmetic: 11.1 us -> none  [the longest x1 6 us: body(): jnp.sum(lax.optimization_barrier(left.astype(jnp.bfloat16)).astype(jnp.fl...]
  transfers between devices with their start and end apart: 8 -> 0, of which waited for: 7 -> 0; matrix products, arithmetic and copies ran while one was open for 18% -> 0% of each run, Pallas kernels for 0% -> 0%
where the time goes in v1:
time: 82.8 us; the launch traced here: 82.5 us
  Pallas kernels  71.3 us (86%)
  local copies, waits for them, and re-layouts  10.6 us (13%)
    pallas_call x1, Pallas kernels, body(): pl.pallas_call(functools.partial(kernel, n_dp, n_ep), out_shape=(jax.Shap...  71.3 us
    unnamed x12, local copies, waits for them, and re-layouts  9.1 us

profile of v1, /device:TPU:0, one launch (start us, length us, event | category | flops | bytes accessed | tf_op | source)
XLA Modules:
  0.0 82.5 jit_solution(9527552628503278958)
XLA Ops:
  0.6 1.4 %copy.13.rw_ref = bf16[128,8]{1,0:T(8,128)(2,1)} copy(bf16[128,8]{0,1:T(8,128)(2,1)} %param.10) | data formatting | bytes 4096 | tf_op args[3]
  2.0 1.4 %copy.12.ids_ref = s32[128,8]{1,0:T(8,128)} copy(s32[128,8]{0,1:T(8,128)} %param.9) | data formatting | bytes 8192 | tf_op args[2]
  3.4 71.3 %shard_map.110 = (bf16[128,7168]{1,0:T(8,128)(2,1)}, f32[128,8]{1,0:T(8,128)}, bf16[1792,256]{1,0:T(8,128)(2,1)}, bf16[1792,256]{1,0:T(8,128)(2,1)}, bf16[1792,256]{1,0:T(8,128)(2,1)}) custom-call(bf16[128,7168]{1,0:T(8,128)(2,1)} %tok_hbm.1, bf16[128,7168]{1,0:T(8,128)(2,1)} %grad_hbm.1, s32[128,8]{1,0:T(8,128)} %copy.12.ids_ref, ...), custom_call_target="tpu_custom_call" | custom-call | tf_op jit(solution)/shard_map/pallas_call | solution.py:321
  74.7 1.5 %copy.14 = f32[128,8]{0,1:T(8,128)} copy(f32[128,8]{1,0:T(8,128)} %get-tuple-element.6) | data formatting | bytes 8192 | tf_op jit(solution)/shard_map/pallas_call | solution.py:321
  76.2 0.0 copy-start.2
  76.2 2.9 %copy.19 = bf16[128,7168]{1,0:T(8,128)(2,1)} copy(bf16[128,7168]{1,0:T(8,128)(2,1)} %get-tuple-element.15) | data formatting | bytes 3670016
  79.1 0.0 copy-done.2
  79.1 0.0 copy-start.1
  79.1 0.0 copy-start
  79.1 0.9 %copy.20 = bf16[1792,256]{1,0:T(8,128)(2,1)} copy(bf16[1792,256]{1,0:T(8,128)(2,1)S(1)} %copy-done.2) | data formatting | bytes 1835008
  80.1 0.6 copy-done.1
  80.6 0.9 %copy.21 = bf16[1792,256]{1,0:T(8,128)(2,1)} copy(bf16[1792,256]{1,0:T(8,128)(2,1)S(1)} %copy-done.1) | data formatting | bytes 1835008
  81.6 0.0 copy-done
  81.6 0.9 %copy.22 = bf16[1792,256]{1,0:T(8,128)(2,1)} copy(bf16[1792,256]{1,0:T(8,128)(2,1)S(1)} %copy-done) | data formatting | bytes 1835008
Async XLA Ops:
  76.2 2.9 %copy-start.2 = (bf16[1792,256]{1,0:T(8,128)(2,1)S(1)}, bf16[1792,256]{1,0:T(8,128)(2,1)}, u32[]{:S(2)}) copy-start(bf16[1792,256]{1,0:T(8,128)(2,1)} %get-tuple-element.17) | copy-start | bytes 2752516
  79.1 1.5 %copy-start.1 = (bf16[1792,256]{1,0:T(8,128)(2,1)S(1)}, bf16[1792,256]{1,0:T(8,128)(2,1)}, u32[]{:S(2)}) copy-start(bf16[1792,256]{1,0:T(8,128)(2,1)} %get-tuple-element.18) | copy-start | bytes 2752516
  79.1 2.4 %copy-start = (bf16[1792,256]{1,0:T(8,128)(2,1)S(1)}, bf16[1792,256]{1,0:T(8,128)(2,1)}, u32[]{:S(2)}) copy-start(bf16[1792,256]{1,0:T(8,128)(2,1)} %get-tuple-element.19) | copy-start | bytes 2752516

commit v2 on v1

v2 whole, which is shorter than its diff:
```python
import functools
import jax
import jax.numpy as jnp
from jax import lax
from jax.experimental import pallas as pl
from jax.experimental.pallas import tpu as pltpu
from jax.sharding import PartitionSpec as P

ROUTED = 256
TOPK = 8
SLICES = 8
CAP = 8
LANES = 128
BF = jnp.bfloat16
F32 = jnp.float32
MESH = pl.DeviceIdType.MESH


def kernel(
    n_dp, n_ep,
    tok_hbm, grad_hbm, ids_ref, rw_ref, a_hbm, b_hbm, c_hbm,
    fin, sel_ref, ga_hbm, gb_hbm, gc_hbm,
    tokbuf, gradbuf, wab, wc, send1, shard, ag, xs, ys, gates, psum, arsend, arrecv,
    deltas, scaleds, rp, r1recv, r2send, r2recv, retbuf, ga, gb, gc,
    in_sem, w_sem, s1s, s1r, s2s, s2d, s2r, sas, s3s, s3r, ars, arr, r1s, r1r, r2s, r2r, fs, fr,
):
    experts = n_ep // SLICES
    stride = ROUTED // experts
    places = experts * CAP
    n_hi = n_ep // 2
    rows, width = tok_hbm.shape
    lw, hid = a_hbm.shape
    nb = n_dp.bit_length() - 1
    chunk = 2 * n_dp * CAP
    half = n_dp * CAP
    g = lax.axis_index("dp")
    e = lax.axis_index("ep")
    hi, lo = e // 2, e % 2
    other = hi * 2 + (1 - lo)
    mine_w = e // SLICES

    def rc(src, dst, ss, rs, **where):
        return pltpu.make_async_remote_copy(
            src_ref=src, dst_ref=dst, send_sem=ss, recv_sem=rs,
            device_id=where, device_id_type=MESH)

    def cols(j):
        gp = lax.rem(g + j, n_dp)
        return gp, pl.ds(pl.multiple_of(gp * lw, LANES), lw)

    order = [n_dp // 2] + [j for j in range(1, n_dp) if j != n_dp // 2] + [0]
    loads = []
    for q, (src, buf) in enumerate(((tok_hbm, tokbuf), (grad_hbm, gradbuf))):
        for j in order:
            gp, ds = cols(j)
            c = pltpu.make_async_copy(src.at[:, ds], buf.at[j], in_sem.at[q, j])
            c.start()
            loads.append((q, j, gp, buf, c))
    wloads = [
        pltpu.make_async_copy(a_hbm, wab.at[:, pl.ds(0, hid)], w_sem.at[0]),
        pltpu.make_async_copy(b_hbm, wab.at[:, pl.ds(hid, hid)], w_sem.at[1]),
        pltpu.make_async_copy(c_hbm, wc, w_sem.at[2]),
    ]

    barrier = pltpu.get_barrier_semaphore()
    for j in range(1, n_dp):
        pl.semaphore_signal(barrier, inc=1, device_id={"dp": lax.rem(g + j, n_dp)}, device_id_type=MESH)
    for j in range(1, n_hi):
        pl.semaphore_signal(
            barrier, inc=1, device_id={"ep": lax.rem(hi + j, n_hi) * 2 + lo}, device_id_type=MESH)
    pl.semaphore_signal(barrier, inc=1, device_id={"ep": other}, device_id_type=MESH)

    pad = jnp.zeros((LANES - TOPK, rows), F32)
    ids = jnp.concatenate([ids_ref[...].astype(F32), pad], axis=0).T
    rw = jnp.concatenate([rw_ref[...].astype(F32), pad], axis=0).T
    lane = lax.broadcasted_iota(jnp.int32, (rows, LANES), 1)
    wanted = jnp.where(lane < places, (lane // CAP) * stride, -1).astype(F32)
    hits = jnp.zeros((rows, LANES), F32)
    wts = jnp.zeros((rows, LANES), F32)
    for k in range(TOPK):
        m = ids[:, k:k + 1] == wanted
        hits = hits + jnp.where(m, 1.0, 0.0)
        wts = wts + jnp.where(m, rw[:, k:k + 1], 0.0)
    tr = lax.broadcasted_iota(jnp.int32, (rows, rows), 0)
    tc = lax.broadcasted_iota(jnp.int32, (rows, rows), 1)
    lower = jnp.where(tc < tr, 1.0, 0.0).astype(BF)
    slot = jnp.dot(lower, hits.astype(BF), preferred_element_type=F32)
    sel = jnp.where(slot == (lane % CAP).astype(F32), hits, 0.0)
    sel_ref[...] = sel
    selT = sel.T[:places].astype(BF)
    gwT = (sel * wts).T[:places].astype(BF)
    gate = jnp.dot(gwT, jnp.ones((rows, LANES), BF), preferred_element_type=F32)
    gate = gate.reshape(experts, CAP, LANES).astype(BF)

    pl.semaphore_wait(barrier, n_dp - 1 + n_hi)

    pieces = (pl.ds(0, lw), pl.ds(lw, lw + LANES))

    def slices(j, q, gp):
        return rc(send1.at[j, :, :, pieces[q]], shard.at[:, g, :, pieces[q]], s1s.at[q, j], s1r.at[q, g], dp=gp)

    for q, j, gp, buf, c in loads:
        c.wait()
        r = jnp.dot(selT, buf[j], preferred_element_type=F32).reshape(experts, CAP, lw).astype(BF)
        if j:
            send1[j, :, :, q * lw:(q + 1) * lw] = r
            if q:
                send1[j, :, :, 2 * lw:] = gate
            slices(j, q, gp).start()
        else:
            shard[:, g, :, q * lw:(q + 1) * lw] = r
            if q:
                shard[:, g, :, 2 * lw:] = gate
    for c in wloads:
        c.start()

    per = SLICES // 2
    pos = hi % per
    base = hi - pos

    def at_order(k):
        m = jnp.where(pos < per - 1 - pos, pos, per - 1 - pos)
        near = jnp.where(k % 2 == 1, pos - (k + 1) // 2, pos + k // 2)
        far = jnp.where(pos < per - 1 - pos, k, per - 1 - k)
        return jnp.where(k <= 2 * m, near, far)

    def seen(h, q):
        return ag.at[h * 2 + lo, :, :, pieces[q]]

    def link(p, v, q, up):
        h = v * per + p
        to = hi + 1 - 2 * up
        return rc(seen(h, q), seen(h, q), (s2d if up else s2s).at[h, q], s2r.at[h, q], ep=to * 2 + lo)

    def link_in(p, v, q):
        h = v * per + p
        return rc(seen(h, q), seen(h, q), s2s.at[h, q], s2r.at[h, q], ep=other)

    def fwd(p, v, q):
        h = v * per + p
        return rc(seen(h, q), seen(h, q), s3s.at[h, q], s3r.at[h, q], ep=other)

    def fwd_in(p, v, q):
        h = v * per + p
        r = ag.at[h * 2 + 1 - lo, :, :, pieces[q]]
        return rc(r, r, s3s.at[h, q], s3r.at[h, q], ep=other)

    def across(i, q):
        h = lax.rem(hi + i * per, n_hi)
        return rc(shard.at[h // per, :, :, pieces[q]], seen(hi, q), sas.at[i, q], s2r.at[hi, q], ep=h * 2 + lo)

    def across_in(i, q):
        h = lax.rem(hi + i * per, n_hi)
        return rc(seen(h, q), seen(h, q), sas.at[i, q], s2r.at[h, q], ep=other)

    def onward(p, v, q, wait):
        @pl.when((p <= pos) & (pos < per - 1))
        def _():
            d = link(p, v, q, 0)
            d.wait_send() if wait else d.start()

        @pl.when((p >= pos) & (pos > 0))
        def _():
            d = link(p, v, q, 1)
            d.wait_send() if wait else d.start()

    for q in range(2):
        for j in range(1, n_dp):
            src = lax.rem(g + j, n_dp)
            rc(send1.at[j, :, :, pieces[q]], shard.at[:, src, :, pieces[q]], s1s.at[q, j], s1r.at[q, src], dp=src).wait_recv()
        for i in range(1, experts):
            across(i, q).start()
        if q:
            ag[e, :, :, lw:] = shard[mine_w, :, :, lw:]
        else:
            ag[e, :, :, :lw] = shard[mine_w, :, :, :lw]
        onward(pos, mine_w, q, False)
        fwd(pos, mine_w, q).start()
        for i in range(1, experts):
            across_in(i, q).wait_recv()
            v = lax.rem(mine_w + i, experts)
            onward(pos, v, q, False)
            fwd(pos, v, q).start()
    for c in wloads:
        c.wait()

    def ar(b, h):
        bit = 1 << b
        peer = g + (1 - 2 * ((g // bit) % 2)) * bit
        return rc(arsend.at[b, h], arrecv.at[b, h], ars.at[b, h], arr.at[b, h], dp=peer)

    def at_chunk(h):
        return pl.ds(pl.multiple_of(h * chunk, 16), chunk)

    def chunk_of(t):
        p, v = at_order(t // experts), t % experts
        return p, v, v * per + p

    def flow(t, carry):
        @pl.when((t >= experts) & (t < n_hi))
        def _():
            p, v, h = chunk_of(t)
            for q in range(2):
                link_in(p, v, q).wait_recv()
                onward(p, v, q, False)
                fwd(p, v, q).start()

        @pl.when((t >= 1) & (t <= n_hi))
        def _():
            p, v, h = chunk_of(t - 1)
            fwd_in(p, v, 0).wait_recv()
            x = ag[pl.ds(h * 2, 2), :, :, 0:lw].astype(F32).reshape(chunk, lw).astype(BF)
            xs[at_chunk(h), :] = x
            p1 = jnp.dot(x, wab[...], preferred_element_type=F32)
            psum[h, :, 0:2 * hid] = p1
            arsend[0, h, :, 0:2 * hid] = p1.astype(BF)
            fwd_in(p, v, 1).wait_recv()
            y = ag[pl.ds(h * 2, 2), :, :, lw:2 * lw].astype(F32).reshape(chunk, lw).astype(BF)
            gates[at_chunk(h), :] = ag[pl.ds(h * 2, 2), :, :, 2 * lw:].astype(F32).reshape(chunk, LANES)
            ys[at_chunk(h), :] = y
            p2 = jnp.dot(y, wc[...], preferred_element_type=F32)
            psum[h, :, 2 * hid:] = p2
            arsend[0, h, :, 2 * hid:] = p2.astype(BF)
            ar(0, h).start()

        for b in range(nb - 1):
            @pl.when((t >= 2 + b) & (t < n_hi + 2 + b))
            def _(b=b):
                p, v, h = chunk_of(t - 2 - b)
                ar(b, h).wait_recv()
                s = psum[h] + arrecv[b, h].astype(F32)
                psum[h] = s
                arsend[b + 1, h] = s.astype(BF)
                ar(b + 1, h).start()
        return carry

    lax.fori_loop(0, n_hi + nb, flow, 0)

    def r1(h):
        return rc(rp.at[h, 1 - lo], r1recv.at[h], r1s.at[h], r1r.at[h], ep=other)

    def finish(i, carry):
        p, v, h = chunk_of(i)
        ar(nb - 1, h).wait_recv()
        s = psum[h] + arrecv[nb - 1, h].astype(F32)
        gate_pre, up_pre, proj = s[:, :hid], s[:, hid:2 * hid], s[:, 2 * hid:]
        scaling = gates[at_chunk(h), 0:1]
        sig = 1.0 / (1.0 + jnp.exp(-gate_pre))
        sw = gate_pre * sig
        hidden = (sw * up_pre).astype(BF).astype(F32)
        route = jnp.sum(hidden * proj, axis=1, keepdims=True)
        gh = scaling * proj
        d1 = (gh * up_pre * sig * (1.0 + gate_pre * (1.0 - sig))).astype(BF)
        d2 = (gh * sw).astype(BF)
        deltas[at_chunk(h), 0:hid] = d1
        deltas[at_chunk(h), hid:] = d2
        scaleds[at_chunk(h), :] = (scaling * hidden).astype(BF)
        part = lax.dot_general(
            jnp.concatenate([d1, d2], axis=1), wab[...], (((1,), (1,)), ((), ())),
            preferred_element_type=F32)
        rp[h, :, :, 0:lw] = part.reshape(2, half, lw).astype(BF)
        rp[h, :, :, lw:] = jnp.broadcast_to(route, (chunk, LANES)).reshape(2, half, LANES).astype(BF)
        r1(h).start()
        return carry

    lax.fori_loop(0, n_hi, finish, 0)

    def r2(h):
        return rc(r2send.at[h], r2recv.at[hi], r2s.at[h], r2r.at[hi], ep=h * 2 + lo)

    def pair(h):
        r1(h).wait_recv()
        return rp[h, lo].astype(F32) + r1recv[h].astype(F32)

    def combine(i, carry):
        h = lax.rem(hi + i, n_hi)
        r2send[h] = pair(h).astype(BF)
        r2(h).start()
        return carry

    lax.fori_loop(1, n_hi, combine, 0)
    r2recv[hi] = pair(hi).astype(BF)

    tile = 256 if lw % 256 == 0 else 128

    def wgrad(i, carry):
        ds = pl.ds(pl.multiple_of(i * tile, LANES), tile)
        dn = (((0,), (0,)), ((), ()))
        both = lax.dot_general(xs[:, ds], deltas[...], dn, preferred_element_type=F32).astype(BF)
        ga[ds, :] = both[:, :hid]
        gb[ds, :] = both[:, hid:]
        gc[ds, :] = lax.dot_general(ys[:, ds], scaleds[...], dn, preferred_element_type=F32).astype(BF)
        return carry

    lax.fori_loop(0, lw // tile, wgrad, 0)
    outs = [
        pltpu.make_async_copy(ga, ga_hbm, w_sem.at[0]),
        pltpu.make_async_copy(gb, gb_hbm, w_sem.at[1]),
        pltpu.make_async_copy(gc, gc_hbm, w_sem.at[2]),
    ]
    for c in outs:
        c.start()

    for i in range(1, n_hi):
        h = lax.rem(hi + i, n_hi)
        rc(r2send.at[h], r2recv.at[h], r2s.at[h], r2r.at[h], ep=h * 2 + lo).wait_recv()
    for w in range(experts):
        acc = r2recv[w * per].astype(F32)
        for j in range(1, per):
            acc = acc + r2recv[w * per + j].astype(F32)
        retbuf[:, w] = acc.reshape(n_dp, CAP, lw + LANES).astype(BF)
    for j in range(1, n_dp):
        gp = lax.rem(g + j, n_dp)
        rc(retbuf.at[gp], fin.at[g], fs.at[j], fr.at[g], dp=gp).start()
    fin[g] = retbuf[g]
    for j in range(1, n_dp):
        gp = lax.rem(g + j, n_dp)
        rc(retbuf.at[gp], fin.at[gp], fs.at[j], fr.at[gp], dp=gp).wait_recv()

    for j in range(1, n_dp):
        gp = lax.rem(g + j, n_dp)
        slices(j, 0, gp).wait_send()
        slices(j, 1, gp).wait_send()
        rc(retbuf.at[gp], fin.at[g], fs.at[j], fr.at[g], dp=gp).wait_send()

    def drain(i, carry):
        h = lax.rem(hi + i, n_hi)
        for q in range(2):
            fwd(h % per, h // per, q).wait_send()
            onward(h % per, h // per, q, True)
        for b in range(nb):
            ar(b, h).wait_send()
        r1(h).wait_send()

        @pl.when(i >= 1)
        def _():
            r2(h).wait_send()
        return carry

    lax.fori_loop(0, n_hi, drain, 0)
    for i in range(1, experts):
        for q in range(2):
            across(i, q).wait_send()
    for c in outs:
        c.wait()


def finish_kernel(
    fin, sel_ref, ids_ref, ga_in, gb_in, gc_in, ig_hbm, rg_ref, ga_out, gb_out, gc_out,
    buf, obuf, sem_in, sem_out, osem,
):
    n_dp, experts, _, wide = fin.shape
    places = experts * CAP
    lw = wide - LANES
    rows = sel_ref.shape[0]
    stride = ROUTED // experts
    ins = [pltpu.make_async_copy(r, buf.at[i], sem_in.at[i]) for i, r in enumerate((ga_in, gb_in, gc_in))]
    outs = [pltpu.make_async_copy(buf.at[i], r, sem_out.at[i]) for i, r in enumerate((ga_out, gb_out, gc_out))]
    for c in ins:
        c.start()
    sel = sel_ref[...]
    selP = sel[:, :places].astype(BF)
    ocopies = []
    for j in range(n_dp):
        vals = fin[j].astype(F32).reshape(places, wide)
        obuf[:, j * lw:(j + 1) * lw] = jnp.dot(
            selP, vals[:, :lw].astype(BF), preferred_element_type=F32).astype(BF)
        ds = pl.ds(j * lw, lw)
        c = pltpu.make_async_copy(obuf.at[:, ds], ig_hbm.at[:, ds], osem.at[j])
        c.start()
        ocopies.append(c)
        if j < 3:
            ins[j].wait()
            outs[j].start()
    vals = fin[0].astype(F32).reshape(places, wide)
    route = jnp.concatenate([vals[:, lw:], jnp.zeros((LANES - places, LANES), F32)], axis=0).T[0:1]
    terms = sel * route
    pad = jnp.zeros((LANES - TOPK, rows), F32)
    ids = jnp.concatenate([ids_ref[...].astype(F32), pad], axis=0).T
    lane = lax.broadcasted_iota(jnp.int32, (rows, LANES), 1)
    wanted = jnp.where(lane < places, (lane // CAP) * stride, -1).astype(F32)
    rg = jnp.zeros((rows, LANES), F32)
    for k in range(TOPK):
        v = jnp.sum(jnp.where(ids[:, k:k + 1] == wanted, terms, 0.0), axis=1, keepdims=True)
        rg = jnp.where(lane == k, v, rg)
    rg_ref[...] = rg.T[:TOPK]
    for c in outs + ocopies:
        c.wait()


def body(tokens, out_grad, expert_ids, route_weights, gate_matrix, up_matrix, down_matrix):
    n_dp, n_ep = lax.axis_size("dp"), lax.axis_size("ep")
    experts = n_ep // SLICES
    n_hi = n_ep // 2
    rows, width = tokens.shape
    lw, hid = gate_matrix.shape
    nb = n_dp.bit_length() - 1
    chunk = 2 * n_dp * CAP
    half = n_dp * CAP
    total = n_hi * chunk
    C = 2 * lw + LANES
    R = lw + LANES
    V = pltpu.VMEM
    D = lambda *s: pltpu.SemaphoreType.DMA(s)
    anyspec = pl.BlockSpec(memory_space=pl.ANY)
    vspec = pl.BlockSpec(memory_space=pltpu.VMEM)
    ids = expert_ids.T
    grad = jax.ShapeDtypeStruct((lw, hid), BF)
    fin, sel, ga, gb, gc = pl.pallas_call(
        functools.partial(kernel, n_dp, n_ep),
        out_shape=(
            jax.ShapeDtypeStruct((n_dp, experts, CAP, R), BF),
            jax.ShapeDtypeStruct((rows, LANES), F32),
            grad, grad, grad,
        ),
        in_specs=[anyspec, anyspec, vspec, vspec, anyspec, anyspec, anyspec],
        out_specs=(vspec, vspec, anyspec, anyspec, anyspec),
        scratch_shapes=[
            V((n_dp, rows, lw), BF), V((n_dp, rows, lw), BF), V((lw, 2 * hid), BF), V((lw, hid), BF),
            V((n_dp, experts, CAP, C), BF), V((experts, n_dp, CAP, C), BF), V((n_ep, n_dp, CAP, C), BF),
            V((total, lw), BF), V((total, lw), BF), V((total, LANES), F32),
            V((n_hi, chunk, 3 * hid), F32), V((nb, n_hi, chunk, 3 * hid), BF), V((nb, n_hi, chunk, 3 * hid), BF),
            V((total, 2 * hid), BF), V((total, hid), BF),
            V((n_hi, 2, half, R), BF), V((n_hi, half, R), BF), V((n_hi, half, R), BF), V((n_hi, half, R), BF),
            V((n_dp, experts, CAP, R), BF),
            V((lw, hid), BF), V((lw, hid), BF), V((lw, hid), BF),
            D(2, n_dp), D(3), D(2, n_dp), D(2, n_dp), D(n_hi, 2), D(n_hi, 2), D(n_hi, 2), D(experts, 2),
            D(n_hi, 2), D(n_hi, 2),
            D(nb, n_hi), D(nb, n_hi), D(n_hi), D(n_hi), D(n_hi), D(n_hi), D(n_dp), D(n_dp),
        ],
        compiler_params=pltpu.CompilerParams(
            collective_id=0, has_side_effects=True, vmem_limit_bytes=67043328),
    )(tokens, out_grad, ids, route_weights.T, gate_matrix, up_matrix, down_matrix)
    ig, rg, ga, gb, gc = pl.pallas_call(
        finish_kernel,
        out_shape=(
            jax.ShapeDtypeStruct((rows, width), BF),
            jax.ShapeDtypeStruct((TOPK, rows), F32),
            grad, grad, grad,
        ),
        in_specs=[vspec, vspec, vspec, anyspec, anyspec, anyspec],
        out_specs=(anyspec, vspec, anyspec, anyspec, anyspec),
        scratch_shapes=[V((3, lw, hid), BF), V((rows, width), BF), D(3), D(3), D(n_dp)],
        compiler_params=pltpu.CompilerParams(vmem_limit_bytes=67043328),
    )(fin, sel, ids, ga, gb, gc)
    return ig, rg.T, ga, gb, gc


def solution(mesh):
    return jax.shard_map(
        body,
        mesh=mesh,
        in_specs=(
            P(("dp", "ep"), None),
            P(("dp", "ep"), None),
            P(("dp", "ep"), None),
            P(("dp", "ep"), None),
            P("dp", "ep"),
            P("dp", "ep"),
            P("dp", "ep"),
        ),
        out_specs=(
            P(("dp", "ep"), None),
            P(("dp", "ep"), None),
            P("dp", "ep"),
            P("dp", "ep"),
            P("dp", "ep"),
        ),
        check_vma=False,
    )
```

time: 82.8 us -> 67.2 us (0.81)
  local copies, waits for them, and re-layouts: 10.6 us -> 0 us
  Pallas kernels: 71.3 us -> 66.2 us
    pallas_call x1, Pallas kernels: 71.3 us -> 61.1 us  [body(): pl.pallas_call(functools.partial(kernel, n_dp, n_ep), out_shape=(jax.Shap...]
    unnamed x12 -> x0, local copies, waits for them, and re-layouts: 9.1 us -> none
    pallas_call x0 -> x1, Pallas kernels: none -> 5.14 us  [body(): pl.pallas_call(finish_kernel, out_shape=(jax.ShapeDtypeStruct((rows, widt...]
    pallas_call x1 -> x0, local copies, waits for them, and re-layouts: 1.5 us -> none  [body(): pl.pallas_call(functools.partial(kernel, n_dp, n_ep), out_shape=(jax.Shap...]
where the time goes in v2:
time: 67.2 us; the launch traced here: 66.9 us
  Pallas kernels  66.2 us (99%)
    pallas_call x1, Pallas kernels, body(): pl.pallas_call(functools.partial(kernel, n_dp, n_ep), out_shape=(jax.Shap...  61.1 us
    pallas_call x1, Pallas kernels, body(): pl.pallas_call(finish_kernel, out_shape=(jax.ShapeDtypeStruct((rows, widt...  5.14 us

profile of v2, /device:TPU:0, one launch (start us, length us, event | category | flops | bytes accessed | tf_op | source)
XLA Modules:
  0.0 66.9 jit_solution(2696300244385879751)
XLA Ops:
  0.6 61.1 %shard_map.110 = (bf16[4,1,8,1920]{3,2,1,0:T(8,128)(2,1)}, f32[128,128]{1,0:T(8,128)}, bf16[1792,256]{1,0:T(8,128)(2,1)}, bf16[1792,256]{1,0:T(8,128)(2,1)}, bf16[1792,256]{1,0:T(8,128)(2,1)}) custom-call(bf16[128,7168]{1,0:T(8,128)(2,1)} %tok_hbm.1, bf16[128,7168]{1,0:T(8,128)(2,1)} %grad_hbm.1, s32[8,128]{1,0:T(8,128)} %bitcast.3, bf16[8,128]{1,0:T(8,128)(2,1)} %bitcast.5, ...), custom_call_target="tpu_custom_call" | custom-call | tf_op jit(solution)/shard_map/pallas_call | solution.py:409
  61.7 5.1 %shard_map.111 = (bf16[128,7168]{1,0:T(8,128)(2,1)}, f32[8,128]{1,0:T(8,128)}, bf16[1792,256]{1,0:T(8,128)(2,1)}, bf16[1792,256]{1,0:T(8,128)(2,1)}, bf16[1792,256]{1,0:T(8,128)(2,1)}) custom-call(bf16[4,1,8,1920]{3,2,1,0:T(8,128)(2,1)} %get-tuple-element.15.fin, f32[128,128]{1,0:T(8,128)} %get-tuple-element.16.sel_ref, s32[8,128]{1,0:T(8,128)} %bitcast.4, ...), custom_call_target="tpu_custom_call" | custom-call | tf_op jit(solution)/shard_map/pallas_call | solution.py:434

commit v3 on v2

--- a/solution.py
+++ b/solution.py
@@ -192,54 +192,14 @@
     def at_chunk(h):
         return pl.ds(pl.multiple_of(h * chunk, 16), chunk)
 
+    def r1(h):
+        return rc(rp.at[h, 1 - lo], r1recv.at[h], r1s.at[h], r1r.at[h], ep=other)
+
     def chunk_of(t):
         p, v = at_order(t // experts), t % experts
         return p, v, v * per + p
 
-    def flow(t, carry):
-        @pl.when((t >= experts) & (t < n_hi))
-        def _():
-            p, v, h = chunk_of(t)
-            for q in range(2):
-                link_in(p, v, q).wait_recv()
-                onward(p, v, q, False)
-                fwd(p, v, q).start()
-
-        @pl.when((t >= 1) & (t <= n_hi))
-        def _():
-            p, v, h = chunk_of(t - 1)
-            fwd_in(p, v, 0).wait_recv()
-            x = ag[pl.ds(h * 2, 2), :, :, 0:lw].astype(F32).reshape(chunk, lw).astype(BF)
-            xs[at_chunk(h), :] = x
-            p1 = jnp.dot(x, wab[...], preferred_element_type=F32)
-            psum[h, :, 0:2 * hid] = p1
-            arsend[0, h, :, 0:2 * hid] = p1.astype(BF)
-            fwd_in(p, v, 1).wait_recv()
-            y = ag[pl.ds(h * 2, 2), :, :, lw:2 * lw].astype(F32).reshape(chunk, lw).astype(BF)
-            gates[at_chunk(h), :] = ag[pl.ds(h * 2, 2), :, :, 2 * lw:].astype(F32).reshape(chunk, LANES)
-            ys[at_chunk(h), :] = y
-            p2 = jnp.dot(y, wc[...], preferred_element_type=F32)
-            psum[h, :, 2 * hid:] = p2
-            arsend[0, h, :, 2 * hid:] = p2.astype(BF)
-            ar(0, h).start()
-
-        for b in range(nb - 1):
-            @pl.when((t >= 2 + b) & (t < n_hi + 2 + b))
-            def _(b=b):
-                p, v, h = chunk_of(t - 2 - b)
-                ar(b, h).wait_recv()
-                s = psum[h] + arrecv[b, h].astype(F32)
-                psum[h] = s
-                arsend[b + 1, h] = s.astype(BF)
-                ar(b + 1, h).start()
-        return carry
-
-    lax.fori_loop(0, n_hi + nb, flow, 0)
-
-    def r1(h):
-        return rc(rp.at[h, 1 - lo], r1recv.at[h], r1s.at[h], r1r.at[h], ep=other)
-
-    def finish(i, carry):
+    def finish(i):
         p, v, h = chunk_of(i)
         ar(nb - 1, h).wait_recv()
         s = psum[h] + arrecv[nb - 1, h].astype(F32)
@@ -261,9 +221,50 @@
         rp[h, :, :, 0:lw] = part.reshape(2, half, lw).astype(BF)
         rp[h, :, :, lw:] = jnp.broadcast_to(route, (chunk, LANES)).reshape(2, half, LANES).astype(BF)
         r1(h).start()
+
+    def flow(t, carry):
+        @pl.when((t >= experts) & (t < n_hi))
+        def _():
+            p, v, h = chunk_of(t)
+            for q in range(2):
+                link_in(p, v, q).wait_recv()
+                onward(p, v, q, False)
+                fwd(p, v, q).start()
+
+        @pl.when((t >= 2) & (t <= n_hi + 1))
+        def _():
+            p, v, h = chunk_of(t - 2)
+            fwd_in(p, v, 0).wait_recv()
+            x = ag[pl.ds(h * 2, 2), :, :, 0:lw].astype(F32).reshape(chunk, lw).astype(BF)
+            xs[at_chunk(h), :] = x
+            p1 = jnp.dot(x, wab[...], preferred_element_type=F32)
+            psum[h, :, 0:2 * hid] = p1
+            arsend[0, h, :, 0:2 * hid] = p1.astype(BF)
+            fwd_in(p, v, 1).wait_recv()
+            y = ag[pl.ds(h * 2, 2), :, :, lw:2 * lw].astype(F32).reshape(chunk, lw).astype(BF)
+            gates[at_chunk(h), :] = ag[pl.ds(h * 2, 2), :, :, 2 * lw:].astype(F32).reshape(chunk, LANES)
+            ys[at_chunk(h), :] = y
+            p2 = jnp.dot(y, wc[...], preferred_element_type=F32)
+            psum[h, :, 2 * hid:] = p2
+            arsend[0, h, :, 2 * hid:] = p2.astype(BF)
+            ar(0, h).start()
+
+        for b in range(nb - 1):
+            @pl.when((t >= 3 + b) & (t < n_hi + 3 + b))
+            def _(b=b):
+                p, v, h = chunk_of(t - 3 - b)
+                ar(b, h).wait_recv()
+                s = psum[h] + arrecv[b, h].astype(F32)
+                psum[h] = s
+                arsend[b + 1, h] = s.astype(BF)
+                ar(b + 1, h).start()
+
+        @pl.when(t >= nb + 2)
+        def _():
+            finish(t - nb - 2)
         return carry
 
-    lax.fori_loop(0, n_hi, finish, 0)
+    lax.fori_loop(0, n_hi + nb + 2, flow, 0)
 
     def r2(h):
         return rc(r2send.at[h], r2recv.at[hi], r2s.at[h], r2r.at[hi], ep=h * 2 + lo)
@@ -272,14 +273,21 @@
         r1(h).wait_recv()
         return rp[h, lo].astype(F32) + r1recv[h].astype(F32)
 
-    def combine(i, carry):
-        h = lax.rem(hi + i, n_hi)
-        r2send[h] = pair(h).astype(BF)
-        r2(h).start()
+    def combine(t, carry):
+        p, v, h = chunk_of(t)
+        both = pair(h).astype(BF)
+
+        @pl.when(h != hi)
+        def _():
+            r2send[h] = both
+            r2(h).start()
+
+        @pl.when(h == hi)
+        def _():
+            r2recv[hi] = both
         return carry
 
-    lax.fori_loop(1, n_hi, combine, 0)
-    r2recv[hi] = pair(hi).astype(BF)
+    lax.fori_loop(0, n_hi, combine, 0)
 
     tile = 256 if lw % 256 == 0 else 128
 
@@ -360,6 +368,9 @@
         c.start()
     sel = sel_ref[...]
     selP = sel[:, :places].astype(BF)
+    for c, o in zip(ins, outs):
+        c.wait()
+        o.start()
     ocopies = []
     for j in range(n_dp):
         vals = fin[j].astype(F32).reshape(places, wide)
@@ -369,9 +380,6 @@
         c = pltpu.make_async_copy(obuf.at[:, ds], ig_hbm.at[:, ds], osem.at[j])
         c.start()
         ocopies.append(c)
-        if j < 3:
-            ins[j].wait()
-            outs[j].start()
     vals = fin[0].astype(F32).reshape(places, wide)
     route = jnp.concatenate([vals[:, lw:], jnp.zeros((LANES - places, LANES), F32)], axis=0).T[0:1]
     terms = sel * route

time: 67.2 us -> 62.8 us (0.935)
  Pallas kernels: 66.2 us -> 61.9 us
    pallas_call x1, Pallas kernels: 61.1 us -> 56.9 us  [body(): pl.pallas_call(functools.partial(kernel, n_dp, n_ep), out_shape=(jax.Shap...]
where the time goes in v3:
time: 62.8 us; the launch traced here: 62.6 us
  Pallas kernels  61.9 us (99%)
  between operations  0.64 us (1%)
    pallas_call x1, Pallas kernels, body(): pl.pallas_call(functools.partial(kernel, n_dp, n_ep), out_shape=(jax.Shap...  56.9 us
    pallas_call x1, Pallas kernels, body(): pl.pallas_call(finish_kernel, out_shape=(jax.ShapeDtypeStruct((rows, widt...  5.06 us

profile of v3, /device:TPU:0, one launch (start us, length us, event | category | flops | bytes accessed | tf_op | source)
XLA Modules:
  0.0 62.6 jit_solution(5973473463302796960)
XLA Ops:
  0.6 56.9 %shard_map.110 = (bf16[4,1,8,1920]{3,2,1,0:T(8,128)(2,1)}, f32[128,128]{1,0:T(8,128)}, bf16[1792,256]{1,0:T(8,128)(2,1)}, bf16[1792,256]{1,0:T(8,128)(2,1)}, bf16[1792,256]{1,0:T(8,128)(2,1)}) custom-call(bf16[128,7168]{1,0:T(8,128)(2,1)} %tok_hbm.1, bf16[128,7168]{1,0:T(8,128)(2,1)} %grad_hbm.1, s32[8,128]{1,0:T(8,128)} %bitcast.3, bf16[8,128]{1,0:T(8,128)(2,1)} %bitcast.5, ...), custom_call_target="tpu_custom_call" | custom-call | tf_op jit(solution)/shard_map/pallas_call | solution.py:417
  57.5 5.1 %shard_map.111 = (bf16[128,7168]{1,0:T(8,128)(2,1)}, f32[8,128]{1,0:T(8,128)}, bf16[1792,256]{1,0:T(8,128)(2,1)}, bf16[1792,256]{1,0:T(8,128)(2,1)}, bf16[1792,256]{1,0:T(8,128)(2,1)}) custom-call(bf16[4,1,8,1920]{3,2,1,0:T(8,128)(2,1)} %get-tuple-element.15.fin, f32[128,128]{1,0:T(8,128)} %get-tuple-element.16.sel_ref, s32[8,128]{1,0:T(8,128)} %bitcast.4, ...), custom_call_target="tpu_custom_call" | custom-call | tf_op jit(solution)/shard_map/pallas_call | solution.py:442
